TPU v7x, 32 devices: a whole 2x2x4 slice. The times are simulated.
32 devices in a mesh: rows: 32 (over z, y, x, core).
Axes of the slice: x: 2, y: 2, z: 4, core: 2. Of those that a mesh axis runs over, the one named last changes fastest.
Arguments:
- snapshots: float32 [16384, 512], P('rows'), may hold values from -100 to 100
- validation: float32 [16384, 512], P('rows'), may hold values from -100 to 100
- eigenvectors: float32 [512, 64], replicated, may hold values from -0.25 to 0.25
- eigenvalues: float32 [64], replicated, may hold values from 16 to 256
Outputs:
- gram: float32 [512, 512], replicated
- modes: float32 [64, 16384], P(None, 'rows')
- train_coef: float32 [64, 512], replicated
- valid_coef: float32 [64, 512], replicated
All inputs are finite; a program needn't handle non-finite values.
Results may differ from a plain program's by a relative error of at most 0.000071.
Values sent between devices are 32-bit elements; how exact they have to be, the bound alone decides.
No kernel may reach another device: no remote copies, remote signals or barrier semaphores. Data moves between devices by JAX's collectives and lax.ppermute only.
A program may use at most 64 MiB of HBM per device.

v0:
```python
import jax
import jax.numpy as jnp
from jax import lax
from jax.sharding import PartitionSpec as P


def body(snapshots, validation, eigenvectors, eigenvalues):
    highest = lax.Precision.HIGHEST
    devices = lax.axis_size("rows")
    total = snapshots.shape[0] * devices * 1.0
    gram_part = (
        lax.dot_general(
            snapshots,
            snapshots,
            (((0,), (0,)), ((), ())),
            precision=highest,
            preferred_element_type=jnp.float32,
        )
        / total
    )
    scales = lax.rsqrt(eigenvalues)
    modes = (
        lax.dot_general(
            eigenvectors,
            snapshots,
            (((0,), (1,)), ((), ())),
            precision=highest,
            preferred_element_type=jnp.float32,
        )
        * scales[:, None]
    )
    gram = lax.psum(gram_part, "rows")
    valid_part = (
        jnp.dot(modes, validation, precision=highest, preferred_element_type=jnp.float32) / total
    )
    valid_coef = lax.psum(valid_part, "rows")
    train_coef = (
        lax.dot_general(
            eigenvectors,
            gram,
            (((0,), (0,)), ((), ())),
            precision=highest,
            preferred_element_type=jnp.float32,
        )
        * scales[:, None]
    )
    return (gram, modes, train_coef, valid_coef)


def solution(mesh):
    in_specs = (P("rows", None), P("rows", None), P(), P())
    out_specs = (P(), P(None, "rows"), P(), P())
    return jax.shard_map(body, mesh=mesh, in_specs=in_specs, out_specs=out_specs, check_vma=False)
```

profile of v0, /device:TPU:0, one launch (start us, length us, event | category | flops | bytes accessed | tf_op | source)
XLA Modules:
  0.0 159.9 jit_solution(1666710015621987377)
XLA Ops:
  7.2 0.0 copy-start
  7.2 0.0 all-reduce.3.cloned.1.call-start
  7.2 0.7 rsqrt.3
  8.0 0.4 copy-done
  8.4 0.0 copy-start.3
  8.4 2.8 %convolution_multiply_fusion = f32[512,512]{1,0:T(8,128)} fusion(f32[512,512]{1,0:T(8,128)S(1)} %copy-done), kind=kOutput, calls=%fused_computation | convolution fusion | flops 1610874880 | bytes 2097152 | tf_op jit(solution)/shard_map/dot_general | solution.py:12
  11.2 0.0 copy-done.3
  11.2 0.0 copy-start.2
  11.2 1.1 convolution_multiply_fusion.3
  12.4 0.1 copy-done.2
  12.5 0.0 copy-start.4
  12.5 1.4 convolution_multiply_fusion.1
  13.9 0.0 copy-done.4
  13.9 0.0 all-reduce.3.cloned.1.call-update
  13.9 134.7 %all-reduce.3.cloned.1.call-done = (f32[512,512]{1,0:T(8,128)}, f32[64,512]{1,0:T(8,128)}) async-done(((f32[512,512]{1,0:T(8,128)}, f32[64,512]{1,0:T(8,128)}), (f32[512,512]{1,0:T(8,128)}, f32[64,512]{1,0:T(8,128)})) %all-reduce.3.cloned.1.call-update) | async-done | bytes 1179664 | tf_op jit(solution)/shard_map/psum | solution.py:32
  148.7 0.0 copy-start.1
  148.7 2.8 %fusion = f32[64,512]{1,0:T(8,128)} fusion(f32[512,512]{1,0:T(8,128)} %get-tuple-element.6, f32[512,64]{0,1:T(8,128)S(1)} %copy-done.3, f32[64]{0:T(128)S(1)} %rsqrt.3), kind=kOutput, calls=%fused_computation.3 | convolution fusion | flops 201359360 | bytes 1310976 | tf_op jit(solution)/shard_map/dot_general | solution.py:38
  151.4 0.0 copy-done.1
  151.4 0.0 copy-start.5
  151.4 1.0 copy.10
  152.4 0.1 copy-done.5
  152.4 0.7 copy.11
Async XLA Ops:
  7.2 1.2 copy-start
  7.2 141.5 %all-reduce.3.cloned.1.call-start = ((), (), s32[]{:S(2)}) async-start(), calls=%async_computation | async-start | bytes 2359296 | tf_op jit(solution)/shard_map/psum | solution.py:32
  8.4 2.8 %copy-start.3 = (f32[512,64]{0,1:T(8,128)S(1)}, f32[512,64]{0,1:T(8,128)}, u32[]{:S(2)}) copy-start(f32[512,64]{0,1:T(8,128)} %param.6) | copy-start | bytes 393220
  11.2 1.2 copy-start.2
  12.5 1.4 copy-start.4
  148.7 2.8 %copy-start.1 = (f32[512,512]{1,0:T(8,128)S(1)}, f32[512,512]{1,0:T(8,128)}, u32[]{:S(2)}) copy-start(f32[512,512]{1,0:T(8,128)} %get-tuple-element.6) | copy-start | bytes 3145732
  151.4 1.0 copy-start.5
Sparse Core Ops, SparseCore 0:
  14.0 134.5 all-reduce.2
where the time goes:
time: 160 us
  waiting for transfers between devices  135 us (84%)
  between operations  14 us (9%)
  matrix products  8.12 us (5%)
  local copies, waits for them, and re-layouts  2.99 us (2%)
    psum x1, waiting for transfers between devices, body(): gram = lax.psum(gram_part, 'rows')  135 us
  transfers between devices with their start and end apart: 1, of which 1 were waited for; matrix products, arithmetic and copies ran while one was open for 0% of the time, Pallas kernels for 0%

commit v1 on v0

--- a/solution.py
+++ b/solution.py
@@ -29,7 +29,8 @@
         )
         * scales[:, None]
     )
-    gram = lax.psum(gram_part, "rows")
+    parts = lax.all_gather(gram_part, "rows", axis=0, tiled=False)
+    gram = parts.sum(axis=0)
     valid_part = (
         jnp.dot(modes, validation, precision=highest, preferred_element_type=jnp.float32) / total
     )

time: 160 us -> 346 us (2.16)
  waiting for transfers between devices: 135 us -> 307 us
  other arithmetic: 0 us -> 12.3 us
    all_gather x0 -> x1, waiting for transfers between devices: none -> 192 us  [body(): parts = lax.all_gather(gram_part, 'rows', axis=0, tiled=False)]
    psum x1, waiting for transfers between devices: 135 us -> 115 us  [body(): valid_coef = lax.psum(valid_part, 'rows')]
    reduce_sum x0 -> x1, other arithmetic: none -> 12.3 us  [body(): gram = parts.sum(axis=0)]
  transfers between devices with their start and end apart: 1 -> 2, of which waited for: 1 -> 2; matrix products, arithmetic and copies ran while one was open for 0% -> 6% of each run, Pallas kernels for 0% -> 0%
where the time goes in v1:
time: 346 us
  waiting for transfers between devices  307 us (89%)
  between operations  14.1 us (4%)
  other arithmetic  12.3 us (4%)
  matrix products  8.98 us (3%)
    all_gather x1, waiting for transfers between devices, body(): parts = lax.all_gather(gram_part, 'rows', axis=0, tiled=False)  192 us
    psum x1, waiting for transfers between devices, body(): valid_coef = lax.psum(valid_part, 'rows')  115 us
    reduce_sum x1, other arithmetic, body(): gram = parts.sum(axis=0)  12.3 us
  transfers between devices with their start and end apart: 2, of which 2 were waited for; matrix products, arithmetic and copies ran while one was open for 6% of the time, Pallas kernels for 0%

profile of v1, /device:TPU:0, one launch (start us, length us, event | category | flops | bytes accessed | tf_op | source)
XLA Modules:
  0.0 345.6 jit_solution(9090806711448041527)
XLA Ops:
  7.2 0.0 copy-start
  7.2 0.0 copy-start.2
  7.2 0.0 all-gather.3.cloned.1.call-start
  7.2 1.2 copy-done
  8.4 2.8 convolution_multiply_fusion
  11.2 0.0 all-gather.3.cloned.1.call-update
  11.3 0.0 all-reduce.2.cloned.1.call-start
  11.3 0.7 rsqrt.3
  12.0 2.0 convolution_multiply_fusion.3
  14.0 0.0 copy-start.3
  14.0 2.7 convolution_multiply_fusion.1
  16.7 0.0 all-reduce.2.cloned.1.call-update
  16.7 191.7 %all-gather.3.cloned.1.call-done = f32[16384,512]{1,0:T(8,128)} async-done(((f32[512,512]{1,0:T(8,128)}), f32[16384,512]{1,0:T(8,128)}) %all-gather.3.cloned.1.call-update) | async-done | bytes 33554448 | tf_op jit(solution)/shard_map/all_gather | solution.py:32
  208.4 12.3 %reduce_sum.9 = f32[512,512]{1,0:T(8,128)S(1)} reduce(f32[32,512,512]{2,1,0:T(8,128)} %bitcast.11, f32[]{:T(128)} %constant.6.clone.1), dimensions={0}, to_apply=%region_0.0 | reduce | flops 8126464 | bytes 34603012 | tf_op jit(solution)/shard_map/reduce_sum | solution.py:33
  220.7 0.0 copy-done.2
  220.7 0.0 copy-start.1
  220.7 1.5 fusion
  222.2 115.0 %all-reduce.2.cloned.1.call-done = f32[64,512]{1,0:T(8,128)} async-done(((f32[64,512]{1,0:T(8,128)}), f32[64,512]{1,0:T(8,128)}) %all-reduce.2.cloned.1.call-update) | async-done | bytes 131088 | tf_op jit(solution)/shard_map/psum | solution.py:37
  337.1 1.6 copy.9
  338.7 0.0 copy-done.3
  338.7 0.0 copy-done.1
Async XLA Ops:
  7.2 1.2 copy-start
  7.2 213.5 %copy-start.2 = (f32[512,64]{0,1:T(8,128)S(1)}, f32[512,64]{0,1:T(8,128)}, u32[]{:S(2)}) copy-start(f32[512,64]{0,1:T(8,128)} %param.6) | copy-start | bytes 393220
  7.2 201.2 %all-gather.3.cloned.1.call-start = ((), (), s32[]{:S(2)}) async-start(), calls=%async_computation.1 | async-start | bytes 34603008 | tf_op jit(solution)/shard_map/all_gather | solution.py:32
  11.3 325.9 %all-reduce.2.cloned.1.call-start = ((), (), s32[]{:S(2)}) async-start(), calls=%async_computation | async-start | bytes 262144 | tf_op jit(solution)/shard_map/psum | solution.py:37
  14.0 324.7 %copy-start.3 = (f32[64,512]{1,0:T(8,128)}, f32[64,512]{1,0:T(8,128)S(1)}, u32[]{:S(2)}) copy-start(f32[64,512]{1,0:T(8,128)S(1)} %convolution_multiply_fusion.3) | copy-start | bytes 393220
  220.7 118.0 %copy-start.1 = (f32[512,512]{1,0:T(8,128)}, f32[512,512]{1,0:T(8,128)S(1)}, u32[]{:S(2)}) copy-start(f32[512,512]{1,0:T(8,128)S(1)} %reduce_sum.9) | copy-start | bytes 3145732
Sparse Core Ops, SparseCore 0:
  11.4 196.9 all-gather.2
  214.5 122.5 all-reduce.1
